TPU v7x, 16 devices: a whole 2x2x2 slice. The times are simulated.
16 devices in a mesh: dp: 2 (over z), emb: 8 (over y, x, core).
Axes of the slice: x: 2, y: 2, z: 2, core: 2. Of those that a mesh axis runs over, the one named last changes fastest.
Arguments:
- tok_ids: int32 [16384], P(('dp', 'emb'))
- resid_in: bfloat16 [16384, 768], P(('dp', 'emb'))
- cot_out: bfloat16 [16384, 768], P(('dp', 'emb'))
- tables: bfloat16 [6, 50304, 768], P(None, 'emb')
- w_up: bfloat16 [6, 768, 3072], replicated
- w_down: bfloat16 [6, 3072, 768], replicated
- w_gate: bfloat16 [6, 768, 768], replicated
- w_proj: bfloat16 [6, 768, 768], replicated
Outputs:
- output 1: bfloat16 [16384, 768], P(('dp', 'emb'))
- output 2: float32 [6, 50304, 768], P(None, 'emb')
All inputs are finite; a program needn't handle non-finite values.
Results may differ from a plain program's by a relative error of at most 0.0151457.
Values are sent between devices in bfloat16 or wider.
A program may use at most 1 GiB of HBM per device.

v0:
```python
import jax
import jax.numpy as jnp
from jax import lax
from jax.sharding import PartitionSpec as P

NORM_EPS = 1e-6


def rms_norm(x_f32):
    return x_f32 * lax.rsqrt(jnp.mean(x_f32 * x_f32, axis=-1, keepdims=True) + NORM_EPS)


def layer_forward(resid_cur, fetched, w_up_l, w_down_l, w_gate_l, w_proj_l):
    x_f32 = resid_cur.astype(jnp.float32)
    normed = rms_norm(x_f32).astype(jnp.bfloat16)
    up_pre = jnp.dot(normed, w_up_l, preferred_element_type=jnp.float32)
    hidden = jax.nn.gelu(up_pre).astype(jnp.bfloat16)
    mlp_out = jnp.dot(hidden, w_down_l, preferred_element_type=jnp.float32)
    gate_pre = jnp.dot(normed, w_gate_l, preferred_element_type=jnp.float32)
    gate_act = jax.nn.gelu(gate_pre)
    mixed_in = (gate_act * fetched.astype(jnp.float32)).astype(jnp.bfloat16)
    proj_out = jnp.dot(mixed_in, w_proj_l, preferred_element_type=jnp.float32)
    resid_next = (x_f32 + mlp_out + proj_out).astype(jnp.bfloat16)
    return resid_next, (resid_cur, up_pre, gate_pre, gate_act, fetched)


def layer_backward(cot_next, layer_saved, w_up_l, w_down_l, w_gate_l, w_proj_l):
    resid_cur, up_pre, gate_pre, gate_act, fetched = layer_saved
    d_mixed = jnp.einsum('td,ed->te', cot_next, w_proj_l, preferred_element_type=jnp.float32).astype(jnp.bfloat16).astype(jnp.float32)
    grad_rows = gate_act * d_mixed
    d_gate_act = d_mixed * fetched.astype(jnp.float32)
    d_gate_pre = jax.vjp(jax.nn.gelu, gate_pre)[1](d_gate_act)[0]
    d_hidden = jnp.einsum('td,fd->tf', cot_next, w_down_l, preferred_element_type=jnp.float32).astype(jnp.bfloat16)
    d_up_pre = jax.vjp(jax.nn.gelu, up_pre)[1](d_hidden.astype(jnp.float32))[0]
    d_norm_mlp = jnp.einsum('tf,df->td', d_up_pre.astype(jnp.bfloat16), w_up_l, preferred_element_type=jnp.float32).astype(jnp.bfloat16)
    d_norm_gate = jnp.einsum('te,de->td', d_gate_pre.astype(jnp.bfloat16), w_gate_l, preferred_element_type=jnp.float32).astype(jnp.bfloat16)
    d_normed = (d_norm_mlp + d_norm_gate).astype(jnp.float32)
    d_x_norm = jax.vjp(rms_norm, resid_cur.astype(jnp.float32))[1](d_normed)[0]
    cot_cur = (cot_next.astype(jnp.float32) + d_x_norm).astype(jnp.bfloat16)
    return cot_cur, grad_rows


def route_plan(tok_ids, range_rows, n_emb, cap_rows):
    owner_ids = tok_ids // range_rows
    local_off = tok_ids - owner_ids * range_rows
    one_hot = (owner_ids[:, None] == jnp.arange(n_emb, dtype=jnp.int32)[None, :]).astype(jnp.int32)
    rank_in = jnp.sum((jnp.cumsum(one_hot, axis=0) - one_hot) * one_hot, axis=1)
    slot_of = owner_ids * cap_rows + rank_in
    tok_count = tok_ids.shape[0]
    slot_token = jnp.zeros((n_emb * cap_rows,), jnp.int32).at[slot_of].set(jnp.arange(tok_count, dtype=jnp.int32))
    slot_mask = jnp.zeros((n_emb * cap_rows,), jnp.float32).at[slot_of].set(1.0)
    send_ids = jnp.where(slot_mask > 0, jnp.take(local_off, slot_token), 0)
    return slot_of, slot_token, slot_mask, send_ids


def solution(mesh):
    n_emb = mesh.shape['emb']
    tok_spec = P(('dp', 'emb'))
    act_spec = P(('dp', 'emb'), None)
    table_spec = P(None, 'emb', None)
    full_spec = P(None, None, None)

    def device_body(tok_ids, resid_in, cot_out, tables, w_up, w_down, w_gate, w_proj):
        n_layers = tables.shape[0]
        range_rows = tables.shape[1]
        tok_count = tok_ids.shape[0]
        cap_rows = min(2 * tok_count // n_emb, 3 * tok_count // 4)
        slot_of, slot_token, slot_mask, send_ids = route_plan(tok_ids, range_rows, n_emb, cap_rows)
        recv_ids = lax.all_to_all(send_ids, 'emb', 0, 0, tiled=True)
        resid_cur = resid_in
        saved_acts = []
        for l_idx in range(n_layers):
            served = jnp.take(tables[l_idx], recv_ids, axis=0)
            returned = lax.all_to_all(served, 'emb', 0, 0, tiled=True)
            fetched = jnp.take(returned, slot_of, axis=0)
            resid_cur, layer_saved = layer_forward(resid_cur, fetched, w_up[l_idx], w_down[l_idx], w_gate[l_idx], w_proj[l_idx])
            saved_acts.append(layer_saved)
        cot_cur = cot_out
        grad_list = [None] * n_layers
        for l_idx in reversed(range(n_layers)):
            cot_cur, grad_rows = layer_backward(cot_cur, saved_acts[l_idx], w_up[l_idx], w_down[l_idx], w_gate[l_idx], w_proj[l_idx])
            outgoing = jnp.take(grad_rows, slot_token, axis=0) * slot_mask[:, None]
            incoming = lax.all_to_all(outgoing, 'emb', 0, 0, tiled=True)
            shard_grad = jax.ops.segment_sum(incoming, recv_ids, num_segments=range_rows)
            grad_list[l_idx] = lax.psum(shard_grad, 'dp')
        return resid_cur, jnp.stack(grad_list)

    return jax.shard_map(device_body, mesh=mesh, in_specs=(tok_spec, act_spec, act_spec, table_spec, full_spec, full_spec, full_spec, full_spec), out_specs=(act_spec, table_spec), check_vma=False)
```

profile of v0, /device:TPU:0, one launch (start us, length us, event | category | flops | bytes accessed | tf_op | source)
XLA Modules:
  0.0 3837.0 jit_solution(6301126215524993147)
XLA Ops:
  35.2 39.0 %slice_bitcast_fusion = (bf16[6288,768]{1,0:T(8,128)(2,1)}, bf16[6288,768]{1,0:T(8,128)(2,1)}, bf16[6288,768]{1,0:T(8,128)(2,1)}, bf16[6288,768]{1,0:T(8,128)(2,...) fusion(bf16[6,6288,768]{2,1,0:T(8,128)(2,1)} %param.17), kind=kLoop, calls=%fused_computation.123 | loop fusion | bytes 115900416 | tf_op jit(solution)/shard_map/squeeze | solution.py:73
  163.6 22.9 broadcast_select_fusion
  203.1 25.5 all-to-all-done.1
  247.7 19.4 fusion.233
  484.9 22.1 fusion.257
  519.6 22.1 fusion.252
  565.3 22.4 fusion.247
  610.9 22.1 fusion.242
  658.1 20.0 fusion.237
  706.0 27.3 select_multiply_fusion
  733.3 77.0 %all_to_all.156 = f32[8,256,768]{2,1,0:T(8,128)} all-to-all(f32[8,256,768]{2,1,0:T(8,128)} %bitcast.324), channel_id=1, replica_groups=mesh['dp'=2,'emb'=8] {'emb'}, dimensions={0} | all-to-all | bytes 12582912 | tf_op jit(solution)/shard_map/all_to_all | solution.py:83
  810.3 75.2 %all_to_all.157 = f32[8,256,768]{2,1,0:T(8,128)} all-to-all(f32[8,256,768]{2,1,0:T(8,128)S(1)} %bitcast.323), channel_id=1, replica_groups=mesh['dp'=2,'emb'=8] {'emb'}, dimensions={0} | all-to-all | bytes 12582912 | tf_op jit(solution)/shard_map/all_to_all | solution.py:83
  885.5 75.2 %all_to_all.158 = f32[8,256,768]{2,1,0:T(8,128)} all-to-all(f32[8,256,768]{2,1,0:T(8,128)S(1)} %bitcast.320), channel_id=1, replica_groups=mesh['dp'=2,'emb'=8] {'emb'}, dimensions={0} | all-to-all | bytes 12582912 | tf_op jit(solution)/shard_map/all_to_all | solution.py:83
  960.7 75.1 %all_to_all.159 = f32[8,256,768]{2,1,0:T(8,128)} all-to-all(f32[8,256,768]{2,1,0:T(8,128)S(1)} %bitcast.317), channel_id=1, replica_groups=mesh['dp'=2,'emb'=8] {'emb'}, dimensions={0} | all-to-all | bytes 12582912 | tf_op jit(solution)/shard_map/all_to_all | solution.py:83
  1035.8 74.8 %all_to_all.160 = f32[8,256,768]{2,1,0:T(8,128)} all-to-all(f32[8,256,768]{2,1,0:T(8,128)S(1)} %bitcast.314), channel_id=1, replica_groups=mesh['dp'=2,'emb'=8] {'emb'}, dimensions={0} | all-to-all | bytes 12582912 | tf_op jit(solution)/shard_map/all_to_all | solution.py:83
  1115.4 23.1 scatter_custom_fusion.2
  1138.5 22.5 scatter_custom_fusion.6
  1160.9 22.7 scatter_custom_fusion.5
  1183.6 22.5 scatter_custom_fusion.4
  1206.1 22.8 scatter_custom_fusion.7
  1228.9 22.6 scatter_custom_fusion.3
  1268.1 2485.1 %all-reduce.3.cloned.1.call-done = (f32[1,6288,768]{2,1,0:T(8,128)}, f32[1,6288,768]{2,1,0:T(8,128)}, f32[1,6288,768]{2,1,0:T(8,128)}, f32[1,6288,768]{2,1,0:T(8...) async-done(((f32[1,6288,768]{2,1,0:T(8,128)}, f32[1,6288,768]{2,1,0:T(8,128)}, f32[1,6288,768]{2,1,0:T(8,128)}, f32[1,6288,768]{2,1,0:T(8,128)}, ...) | async-done | bytes 115900432 | tf_op jit(solution)/shard_map/psum | solution.py:85
  3753.2 16.8 constant_dynamic-update-slice_fusion.5
  3794.3 17.2 constant_dynamic-update-slice_fusion.2
  (286 shorter events, 546.4 us)
Async XLA Ops:
  11.4 640.5 %copy-start.51 = (pred[1024]{0:T(1024)(128)(4,1)}, pred[1024]{0:T(1024)(128)(4,1)S(1)}, u32[]{:S(2)}) copy-start(pred[1024]{0:T(1024)(128)(4,1)S(1)} %get-tuple-element.17) | copy-start | bytes 3076
  29.3 44.8 %all-to-all-start = ((s32[8,256,1]{1,2,0:T(1,128)}), s32[8,256,1]{1,2,0:T(1,128)S(1)}, u32[]{:S(2)}, u32[]{:S(2)}) async-start(s32[8,256,1]{1,2,0:T(1,128)} %bitcast.5), calls=%async_computation | async-start | bytes 16384 | tf_op jit(solution)/shard_map/all_to_all | solution.py:69
  186.5 42.0 %all-to-all-start.1 = ((bf16[8,256,768]{2,1,0:T(8,128)(2,1)}), bf16[8,256,768]{2,1,0:T(8,128)(2,1)S(1)}, u32[]{:S(2)}, u32[]{:S(2)}) async-start(bf16[8,256,768]{2,1,0:T(8,128)(2,1)} %bitcast.336), calls=%async_computation.1 | async-start | bytes 6291456 | tf_op jit(solution)/shard_map/all_to_all | solution.py:74
  230.2 52.3 %all-to-all-start.2 = ((bf16[8,256,768]{2,1,0:T(8,128)(2,1)}), bf16[8,256,768]{2,1,0:T(8,128)(2,1)S(1)}, u32[]{:S(2)}, u32[]{:S(2)}) async-start(bf16[8,256,768]{2,1,0:T(8,128)(2,1)} %bitcast.335), calls=%async_computation.2 | async-start | bytes 6291456 | tf_op jit(solution)/shard_map/all_to_all | solution.py:74
  282.5 42.2 %all-to-all-start.3 = ((bf16[8,256,768]{2,1,0:T(8,128)(2,1)}), bf16[8,256,768]{2,1,0:T(8,128)(2,1)}, u32[]{:S(2)}, u32[]{:S(2)}) async-start(bf16[8,256,768]{2,1,0:T(8,128)(2,1)} %bitcast.334), calls=%async_computation.3 | async-start | bytes 6291456 | tf_op jit(solution)/shard_map/all_to_all | solution.py:74
  324.7 42.2 %all-to-all-start.4 = ((bf16[8,256,768]{2,1,0:T(8,128)(2,1)}), bf16[8,256,768]{2,1,0:T(8,128)(2,1)S(1)}, u32[]{:S(2)}, u32[]{:S(2)}) async-start(bf16[8,256,768]{2,1,0:T(8,128)(2,1)} %bitcast.333), calls=%async_computation.4 | async-start | bytes 6291456 | tf_op jit(solution)/shard_map/all_to_all | solution.py:74
  368.6 42.8 %all-to-all-start.5 = ((bf16[8,256,768]{2,1,0:T(8,128)(2,1)}), bf16[8,256,768]{2,1,0:T(8,128)(2,1)S(1)}, u32[]{:S(2)}, u32[]{:S(2)}) async-start(bf16[8,256,768]{2,1,0:T(8,128)(2,1)} %bitcast.332), calls=%async_computation.5 | async-start | bytes 6291456 | tf_op jit(solution)/shard_map/all_to_all | solution.py:74
  411.4 42.6 %all-to-all-start.6 = ((bf16[8,256,768]{2,1,0:T(8,128)(2,1)}), bf16[8,256,768]{2,1,0:T(8,128)(2,1)}, u32[]{:S(2)}, u32[]{:S(2)}) async-start(bf16[8,256,768]{2,1,0:T(8,128)(2,1)} %bitcast.331), calls=%async_computation.6 | async-start | bytes 6291456 | tf_op jit(solution)/shard_map/all_to_all | solution.py:74
  733.3 77.0 %slice-start.6 = ((s8[6291456]{0:T(1024)(128)(4,1)}), s8[4194304]{0:T(1024)(128)(4,1)S(1)}, s32[]{:S(2)}) async-start(s8[6291456]{0:T(1024)(128)(4,1)} %bitcast.321), calls=%async_computation.20 | async-start | bytes 8388608
  733.3 77.0 %slice-start.7 = ((s8[6291456]{0:T(1024)(128)(4,1)}), s8[2097152]{0:T(1024)(128)(4,1)S(1)}, s32[]{:S(2)}) async-start(s8[6291456]{0:T(1024)(128)(4,1)} %bitcast.321), calls=%async_computation.21 | async-start | bytes 4194304
  810.3 75.2 %slice-start.4 = ((s8[6291456]{0:T(1024)(128)(4,1)}), s8[4194304]{0:T(1024)(128)(4,1)S(1)}, s32[]{:S(2)}) async-start(s8[6291456]{0:T(1024)(128)(4,1)} %bitcast.318), calls=%async_computation.18 | async-start | bytes 8388608
  810.3 75.2 %slice-start.5 = ((s8[6291456]{0:T(1024)(128)(4,1)}), s8[2097152]{0:T(1024)(128)(4,1)S(1)}, s32[]{:S(2)}) async-start(s8[6291456]{0:T(1024)(128)(4,1)} %bitcast.318), calls=%async_computation.19 | async-start | bytes 4194304
  885.5 75.2 %slice-start.2 = ((s8[6291456]{0:T(1024)(128)(4,1)}), s8[4194304]{0:T(1024)(128)(4,1)S(1)}, s32[]{:S(2)}) async-start(s8[6291456]{0:T(1024)(128)(4,1)} %bitcast.315), calls=%async_computation.16 | async-start | bytes 8388608
  885.5 75.2 %slice-start.3 = ((s8[6291456]{0:T(1024)(128)(4,1)}), s8[2097152]{0:T(1024)(128)(4,1)S(1)}, s32[]{:S(2)}) async-start(s8[6291456]{0:T(1024)(128)(4,1)} %bitcast.315), calls=%async_computation.17 | async-start | bytes 4194304
  960.6 75.2 %slice-start = ((s8[6291456]{0:T(1024)(128)(4,1)}), s8[4194304]{0:T(1024)(128)(4,1)S(1)}, s32[]{:S(2)}) async-start(s8[6291456]{0:T(1024)(128)(4,1)} %bitcast.312), calls=%async_computation.14 | async-start | bytes 8388608
  960.7 75.2 %slice-start.1 = ((s8[6291456]{0:T(1024)(128)(4,1)}), s8[2097152]{0:T(1024)(128)(4,1)S(1)}, s32[]{:S(2)}) async-start(s8[6291456]{0:T(1024)(128)(4,1)} %bitcast.312), calls=%async_computation.15 | async-start | bytes 4194304
  1110.6 118.3 %all-to-all-start.8 = ((f32[8,256,768]{2,1,0:T(8,128)}), f32[8,256,768]{2,1,0:T(8,128)}, u32[]{:S(2)}, u32[]{:S(2)}) async-start(f32[8,256,768]{2,1,0:T(8,128)} %bitcast.311), calls=%async_computation.8 | async-start | bytes 12582912 | tf_op jit(solution)/shard_map/all_to_all | solution.py:83
  1115.3 2637.9 %all-reduce.3.cloned.1.call-start = ((), (), s32[]{:S(2)}) async-start(), calls=%async_computation.13 | async-start | bytes 231800832 | tf_op jit(solution)/shard_map/psum | solution.py:85
  3753.2 28.7 slice-start.18
  3753.2 28.7 slice-start.19
  3753.2 28.7 slice-start.20
  3794.3 27.0 slice-start.8
  3794.3 27.0 slice-start.9
  3794.3 27.0 slice-start.10
  (70 other events, 679.9 us)
Sparse Core Ops, SparseCore 0:
  1251.6 2501.5 all-reduce.2
where the time goes:
time: 3840 us
  waiting for transfers between devices  2510 us (65%)
  blocking collectives  377 us (10%)
  matrix products  350 us (9%)
  local copies, waits for them, and re-layouts  337 us (9%)
  other arithmetic  206 us (5%)
    psum x1, waiting for transfers between devices, device_body(): grad_list[l_idx] = lax.psum(shard_grad, 'dp')  2490 us
    all_to_all x5, blocking collectives, device_body(): incoming = lax.all_to_all(outgoing, 'emb', 0, 0, tiled=True)  377 us
    scatter-add x6, other arithmetic, device_body(): jax.ops.segment_sum(incoming, recv_ids, num_segments=range_rows)  136 us
    dot_general x5, matrix products, layer_backward(): jnp.einsum('tf,df->td', d_up_pre.astype(jnp.bfloat16), w_up_l, preferred_...  109 us
    gather x6, local copies, waits for them, and re-layouts, device_body(): served = jnp.take(tables[l_idx], recv_ids, axis=0)  88.8 us
    unnamed x178, local copies, waits for them, and re-layouts  82 us
  transfers between devices with their start and end apart: 9, of which 4 were waited for; matrix products, arithmetic and copies ran while one was open for 10% of the time, Pallas kernels for 0%

commit v1 on v0

v1 whole, which is shorter than its diff:
```python
import jax
import jax.numpy as jnp
from jax import lax
from jax.experimental import pallas as pl
from jax.experimental.pallas import tpu as pltpu
from jax.sharding import PartitionSpec as P


NORM_EPS = 1e-6
GELU_C = 0.7978845608028654
GELU_A = 0.044715
TILE = 256
BLK = 256
GBLK = 512
FCH = 768
F32 = jnp.float32
BF16 = jnp.bfloat16
SENT = 8191


def gelu_and_grad(x):
    x2 = x * x
    t = jnp.tanh(x * (GELU_C + (GELU_C * GELU_A) * x2))
    h = 0.5 + 0.5 * t
    grad = h + (0.5 * x) * (1.0 - t * t) * (GELU_C + (3.0 * GELU_C * GELU_A) * x2)
    return x * h, grad


def nn(a, b):
    return lax.dot_general(a, b, (((1,), (0,)), ((), ())), preferred_element_type=F32)


def nt(a, b):
    return lax.dot_general(a, b, (((1,), (1,)), ((), ())), preferred_element_type=F32)


def norm_stats(xf):
    return lax.rsqrt(jnp.mean(xf * xf, axis=-1, keepdims=True) + NORM_EPS)


def permute_kernel(n_ref, slot_ref, src_ref, out_ref, acc_ref):
    n_slots = src_ref.shape[0]

    @pl.when(pl.program_id(0) < n_ref[0])
    def _():
        slot = slot_ref[...]
        chunk = 512
        acc_ref[...] = jnp.zeros_like(acc_ref)
        for c in range(n_slots // chunk):
            cols = lax.broadcasted_iota(jnp.int32, (TILE, chunk), 1) + c * chunk
            sel = jnp.where(slot == cols, 1.0, 0.0).astype(BF16)
            acc_ref[...] += nn(sel, src_ref[c * chunk:(c + 1) * chunk, :])
        out_ref[...] = acc_ref[...].astype(BF16)


def permute(n_tiles, slot_col, src):
    n_slots, width = src.shape
    tile = lambda i, n: (jnp.minimum(i, n[0] - 1), 0)
    return pl.pallas_call(
        permute_kernel,
        grid_spec=pltpu.PrefetchScalarGridSpec(
            num_scalar_prefetch=1,
            grid=(n_slots // TILE,),
            in_specs=[
                pl.BlockSpec((TILE, 1), tile),
                pl.BlockSpec((n_slots, width), lambda i, n: (0, 0), pipeline_mode=pl.Buffered(1)),
            ],
            out_specs=pl.BlockSpec((TILE, width), tile),
            scratch_shapes=[pltpu.VMEM((TILE, width), F32)],
        ),
        out_shape=jax.ShapeDtypeStruct((n_slots, width), BF16),
        compiler_params=pltpu.CompilerParams(dimension_semantics=("arbitrary",)),
        name="permute",
    )(n_tiles, slot_col, src)


def gather_kernel(n_ref, lo_ref, hi_ref, ids_ref, table_ref, out_ref, acc_ref):
    range_rows = table_ref.shape[1]

    def tile_step(i, carry):
        rows = pl.ds(pl.multiple_of(i * TILE, TILE), TILE)
        ids = ids_ref[rows, :]

        def part(b):
            start = pl.multiple_of(jnp.minimum(b * GBLK, range_rows - GBLK), 16)
            cols = lax.broadcasted_iota(jnp.int32, (TILE, GBLK), 1) + start
            sel = jnp.where((ids == cols) & (cols >= b * GBLK), 1.0, 0.0).astype(BF16)
            return nn(sel, table_ref[0, pl.ds(start, GBLK), :])

        acc_ref[...] = part(lo_ref[i])

        def step(b, c):
            acc_ref[...] += part(b)
            return c

        lax.fori_loop(lo_ref[i] + 1, hi_ref[i] + 1, step, 0)
        out_ref[0, rows, :] = acc_ref[...].astype(BF16)
        return carry

    lax.fori_loop(0, n_ref[0], tile_step, 0)


def gather(n_tiles, lo, hi, ids_col, tables):
    n_layers, range_rows, e = tables.shape
    n_slots = ids_col.shape[0]
    return pl.pallas_call(
        gather_kernel,
        grid_spec=pltpu.PrefetchScalarGridSpec(
            num_scalar_prefetch=3,
            grid=(n_layers,),
            in_specs=[
                pl.BlockSpec((n_slots, 1), lambda l, *_: (0, 0)),
                pl.BlockSpec((1, range_rows, e), lambda l, *_: (l, 0, 0)),
            ],
            out_specs=pl.BlockSpec((1, n_slots, e), lambda l, *_: (l, 0, 0)),
            scratch_shapes=[pltpu.VMEM((TILE, e), F32)],
        ),
        out_shape=jax.ShapeDtypeStruct((n_layers, n_slots, e), BF16),
        compiler_params=pltpu.CompilerParams(dimension_semantics=("arbitrary",)),
        cost_estimate=pl.CostEstimate(flops=60_000_000_000, bytes_accessed=80_000_000, transcendentals=0),
        name="gather",
    )(n_tiles, lo, hi, ids_col, tables)


def weight_copies(hbm, bufs, sems, layer, slot):
    return [pltpu.make_async_copy(h.at[layer], v.at[slot], sems.at[slot, k]) for k, (h, v) in enumerate(zip(hbm, bufs))]


def next_weights(hbm, bufs, sems, step, n_steps, layer_of):
    slot = lax.rem(step, 2)

    @pl.when(step == 0)
    def _():
        for c in weight_copies(hbm, bufs, sems, layer_of(step), slot):
            c.start()

    for c in weight_copies(hbm, bufs, sems, layer_of(step), slot):
        c.wait()

    @pl.when(step + 1 < n_steps)
    def _():
        for c in weight_copies(hbm, bufs, sems, layer_of(step + 1), 1 - slot):
            c.start()


def weight_scratch(d, ffn, e):
    return [
        pltpu.VMEM((2, d, ffn), BF16),
        pltpu.VMEM((2, ffn, d), BF16),
        pltpu.VMEM((2, d, e), BF16),
        pltpu.VMEM((2, e, d), BF16),
        pltpu.SemaphoreType.DMA((2, 4)),
    ]


def fwd_kernel(n_ref, *refs):
    @pl.when(pl.program_id(1) < n_ref[0])
    def _():
        fwd_tile(*refs)


def fwd_tile(x0_ref, e_ref, w_up, w_down, w_gate, w_proj, xs_ref, g_ref, ge_ref, ug_ref, xl_ref,
             x_scr, m_scr, up_buf, down_buf, gate_buf, proj_buf, w_sems):
    l = pl.program_id(0)
    i = pl.program_id(1)
    n_layers = pl.num_programs(0)
    slot = lax.rem(l, 2)
    rows = pl.ds(pl.multiple_of(i * TILE, TILE), TILE)

    @pl.when(i == 0)
    def _():
        next_weights((w_up, w_down, w_gate, w_proj), (up_buf, down_buf, gate_buf, proj_buf), w_sems, l, n_layers, lambda q: q)

    @pl.when(l == 0)
    def _():
        x_scr[rows, :] = x0_ref[...]

    x = x_scr[rows, :]
    xs_ref[0] = x
    xf = x.astype(F32)
    u = (xf * norm_stats(xf)).astype(BF16)
    gate, gate_grad = gelu_and_grad(nn(u, gate_buf[slot]))
    emb = e_ref[0].astype(F32)
    g_ref[0] = gate
    ge_ref[0] = gate_grad * emb
    m_scr[...] = xf + nn((gate * emb).astype(BF16), proj_buf[slot])
    ffn = up_buf.shape[2]
    for c in range(ffn // FCH):
        cs = slice(c * FCH, (c + 1) * FCH)
        hid, hid_grad = gelu_and_grad(nn(u, up_buf[slot, :, cs]))
        ug_ref[0, :, cs] = hid_grad
        m_scr[...] += nn(hid.astype(BF16), down_buf[slot, cs, :])
    x_next = m_scr[...].astype(BF16)
    x_scr[rows, :] = x_next

    @pl.when(l == n_layers - 1)
    def _():
        xl_ref[...] = x_next


def forward(n_tiles, x0, es, w_up, w_down, w_gate, w_proj):
    n_layers, n_slots, e = es.shape
    d = x0.shape[1]
    ffn = w_up.shape[2]
    tile = lambda l, i, n: (l, jnp.minimum(i, n[0] - 1), 0)
    only = lambda which: (lambda l, i, n: (jnp.where(l == which, jnp.minimum(i, n[0] - 1), 0), 0))
    return pl.pallas_call(
        fwd_kernel,
        grid_spec=pltpu.PrefetchScalarGridSpec(
            num_scalar_prefetch=1,
            grid=(n_layers, n_slots // TILE),
            in_specs=[
                pl.BlockSpec((TILE, d), only(0)),
                pl.BlockSpec((1, TILE, e), tile),
            ] + [pl.BlockSpec(memory_space=pl.ANY)] * 4,
            out_specs=[
                pl.BlockSpec((1, TILE, d), tile),
                pl.BlockSpec((1, TILE, e), tile),
                pl.BlockSpec((1, TILE, e), tile),
                pl.BlockSpec((1, TILE, ffn), tile),
                pl.BlockSpec((TILE, d), only(n_layers - 1)),
            ],
            scratch_shapes=[
                pltpu.VMEM((n_slots, d), BF16),
                pltpu.VMEM((TILE, d), F32),
            ] + weight_scratch(d, ffn, e),
        ),
        out_shape=[
            jax.ShapeDtypeStruct((n_layers, n_slots, d), BF16),
            jax.ShapeDtypeStruct((n_layers, n_slots, e), F32),
            jax.ShapeDtypeStruct((n_layers, n_slots, e), F32),
            jax.ShapeDtypeStruct((n_layers, n_slots, ffn), F32),
            jax.ShapeDtypeStruct((n_slots, d), BF16),
        ],
        compiler_params=pltpu.CompilerParams(dimension_semantics=("arbitrary", "arbitrary"), vmem_limit_bytes=66_000_000),
        name="forward",
    )(n_tiles, x0, es, w_up, w_down, w_gate, w_proj)


def bwd_kernel(n_ref, *refs):
    @pl.when(pl.program_id(1) < n_ref[0])
    def _():
        bwd_tile(n_ref[0], *refs)


def bwd_tile(n_tiles, lo_ref, hi_ref, cs_ref, ws_ref, cot_ref, ids_ref, xs_ref, g_ref, ge_ref, ug_ref, w_up, w_down, w_gate, w_proj,
             dt_ref, dx_scr, acc, m_scr, parts_scr, up_buf, down_buf, gate_buf, proj_buf, w_sems, out_sems):
    s = pl.program_id(0)
    i = pl.program_id(1)
    n_layers = pl.num_programs(0)
    l = n_layers - 1 - s
    slot = lax.rem(s, 2)
    rows = pl.ds(pl.multiple_of(i * TILE, TILE), TILE)
    range_rows = dt_ref.shape[1]
    n_blk = acc.shape[0] // BLK
    tail = range_rows - (n_blk - 1) * BLK

    @pl.when(i == 0)
    def _():
        next_weights((w_up, w_down, w_gate, w_proj), (up_buf, down_buf, gate_buf, proj_buf), w_sems, s, n_layers, lambda q: n_layers - 1 - q)

    @pl.when(s == 0)
    def _():
        dx_scr[rows, :] = cot_ref[...]

    dx = dx_scr[rows, :]
    d_mixed = nt(dx, proj_buf[slot]).astype(BF16).astype(F32)
    grad_rows = g_ref[0] * d_mixed
    hi_part = grad_rows.astype(BF16)
    rest = grad_rows - hi_part.astype(F32)
    mid_part = rest.astype(BF16)
    parts_scr[0:TILE, :] = hi_part
    parts_scr[TILE:2 * TILE, :] = mid_part
    parts_scr[2 * TILE:3 * TILE, :] = (rest - mid_part.astype(F32)).astype(BF16)

    @pl.when(l > 0)
    def _():
        d_gate_pre = (ge_ref[0] * d_mixed).astype(BF16)
        d_norm_gate = nt(d_gate_pre, gate_buf[slot]).astype(BF16)
        ffn = up_buf.shape[2]
        for c in range(ffn // FCH):
            cs = slice(c * FCH, (c + 1) * FCH)
            d_hid = nt(dx, down_buf[slot, cs, :]).astype(BF16).astype(F32)
            part = nt((ug_ref[0, :, cs] * d_hid).astype(BF16), up_buf[slot, :, cs])
            if c == 0:
                m_scr[...] = part
            else:
                m_scr[...] += part
        xf = xs_ref[0].astype(F32)
        r = norm_stats(xf)
        d_normed = (m_scr[...].astype(BF16) + d_norm_gate).astype(F32)
        dot_xd = jnp.mean(xf * d_normed, axis=-1, keepdims=True)
        d_x = r * d_normed - xf * (r * r * r * dot_xd)
        dx_scr[rows, :] = (dx.astype(F32) + d_x).astype(BF16)

    def block_copy(b, size):
        at = pl.ds(pl.multiple_of(b * BLK, BLK), size)
        return pltpu.make_async_copy(acc.at[at], dt_ref.at[l, at], out_sems.at[b])

    def each_block(first, last, act):
        def step(b, carry):
            act(block_copy(b, BLK))
            return carry

        lax.fori_loop(first, jnp.minimum(last, n_blk - 1), step, 0)

        @pl.when((first < n_blk) & (last == n_blk))
        def _():
            act(block_copy(n_blk - 1, tail))

    @pl.when((s == 0) & (i == 0))
    def _():
        acc[...] = jnp.zeros_like(acc)

    fresh = ws_ref[i]

    @pl.when(s > 0)
    def _():
        each_block(fresh, ws_ref[i + 1], lambda c: c.wait())

    ids = ids_ref[0]

    def scatter_step(b, carry):
        pos = lax.broadcasted_iota(jnp.int32, (BLK, TILE), 0) + b * BLK
        sel = jnp.where(ids == pos, 1.0, 0.0).astype(BF16)
        part = nn(jnp.concatenate([sel, sel, sel], axis=1), parts_scr[...])
        at = pl.ds(pl.multiple_of(b * BLK, BLK), BLK)

        @pl.when(b >= fresh)
        def _():
            acc[at, :] = part

        @pl.when(b < fresh)
        def _():
            acc[at, :] += part

        return carry

    lax.fori_loop(lo_ref[i], hi_ref[i] + 1, scatter_step, 0)
    each_block(cs_ref[i], cs_ref[i + 1], lambda c: c.start())

    @pl.when((l == 0) & (i == n_tiles - 1))
    def _():
        each_block(0, n_blk, lambda c: c.wait())


def backward(n_tiles, lo, hi, cot, ids_row, xs, g, ge, ug, w_up, w_down, w_gate, w_proj, range_rows):
    n_layers, n_slots, d = xs.shape
    e = g.shape[2]
    ffn = w_up.shape[2]
    top = n_layers - 1
    n_blk = pl.cdiv(range_rows, BLK)
    index = jnp.arange(n_slots // TILE + 1, dtype=jnp.int32)
    copy_start = jnp.where(index == 0, 0, jnp.where(index < n_tiles[0], jnp.append(lo, 0), n_blk)).astype(jnp.int32)
    wait_start = jnp.where(index == 0, 0, jnp.where(index < n_tiles[0], jnp.append(0, hi) + 1, n_blk)).astype(jnp.int32)
    tile = lambda s, i, n, *_: (top - s, jnp.minimum(i, n[0] - 1), 0)
    only = lambda which: (lambda s, i, n, *_: (jnp.where(s == which, jnp.minimum(i, n[0] - 1), 0), 0))
    return pl.pallas_call(
        bwd_kernel,
        grid_spec=pltpu.PrefetchScalarGridSpec(
            num_scalar_prefetch=5,
            grid=(n_layers, n_slots // TILE),
            in_specs=[
                pl.BlockSpec((TILE, d), only(0)),
                pl.BlockSpec((1, 1, TILE), lambda s, i, n, *_: (jnp.minimum(i, n[0] - 1), 0, 0)),
                pl.BlockSpec((1, TILE, d), tile),
                pl.BlockSpec((1, TILE, e), tile),
                pl.BlockSpec((1, TILE, e), tile),
                pl.BlockSpec((1, TILE, ffn), tile),
            ] + [pl.BlockSpec(memory_space=pl.ANY)] * 4,
            out_specs=pl.BlockSpec(memory_space=pl.ANY),
            scratch_shapes=[
                pltpu.VMEM((n_slots, d), BF16),
                pltpu.VMEM((n_blk * BLK, e), F32),
                pltpu.VMEM((TILE, d), F32),
                pltpu.VMEM((3 * TILE, e), BF16),
            ] + weight_scratch(d, ffn, e) + [pltpu.SemaphoreType.DMA((n_blk,))],
        ),
        out_shape=jax.ShapeDtypeStruct((n_layers, range_rows, e), F32),
        compiler_params=pltpu.CompilerParams(dimension_semantics=("arbitrary", "arbitrary"), vmem_limit_bytes=66_000_000),
        name="backward",
    )(n_tiles, lo, hi, copy_start, wait_start, cot, ids_row, xs, g, ge, ug, w_up, w_down, w_gate, w_proj)


def solution(mesh):
    n_dp = mesh.shape['dp']
    n_emb = mesh.shape['emb']
    tok_spec = P(('dp', 'emb'))
    act_spec = P(('dp', 'emb'), None)
    table_spec = P(None, 'emb', None)
    full_spec = P(None, None, None)

    def whole_step(tok_ids, resid_in, cot_out, tables, w_up, w_down, w_gate, w_proj):
        range_rows = tables.shape[1]
        tok_count, _ = resid_in.shape
        cap = 2 * tok_count // n_emb
        send_slots = n_emb * cap
        n_slots = n_dp * send_slots

        owner = tok_ids // range_rows
        local_off = tok_ids - owner * range_rows
        one_hot = (owner[:, None] == jnp.arange(n_emb, dtype=jnp.int32)[None, :]).astype(jnp.int32)
        rank_in = jnp.sum((jnp.cumsum(one_hot, axis=0) - one_hot) * one_hot, axis=1)
        slot_of = owner * cap + rank_in
        match = slot_of[None, :] == jnp.arange(send_slots, dtype=jnp.int32)[:, None]
        slot_ids = jnp.min(jnp.where(match, local_off[None, :], SENT), axis=1)
        sel = match.astype(BF16)

        def exchange(a):
            return lax.all_to_all(jnp.concatenate([a] * n_dp, axis=0), ('dp', 'emb'), 0, 0, tiled=True)

        recv_ids = exchange(slot_ids)
        x_slots = exchange(nn(sel, resid_in).astype(BF16))
        cot_slots = exchange(nn(sel, cot_out).astype(BF16))

        raw_key = recv_ids * n_slots + jnp.arange(n_slots, dtype=jnp.int32)
        key = lax.sort(raw_key)
        slot_sorted = key % n_slots
        ids_sorted = key // n_slots
        count = jnp.sum((recv_ids < range_rows).astype(jnp.int32))
        n_tiles = ((count + TILE - 1) // TILE)[None]
        by_tile = ids_sorted.reshape(n_slots // TILE, TILE)
        lo = by_tile[:, 0]
        hi = jnp.max(jnp.where(by_tile < range_rows, by_tile, 0), axis=1)
        own_key = lax.dynamic_slice(raw_key, (lax.axis_index('dp') * send_slots,), (send_slots,))
        own_pos = jnp.sum((raw_key[None, :] < own_key[:, None]).astype(jnp.int32), axis=1)
        slot_col = slot_sorted[:, None]

        es = gather(n_tiles, lo // GBLK, hi // GBLK, ids_sorted[:, None], tables)
        x0 = permute(n_tiles, slot_col, x_slots)
        xs, g, ge, ug, x_last = forward(n_tiles, x0, es, w_up, w_down, w_gate, w_proj)
        back = lax.all_to_all(jnp.take(x_last, own_pos, axis=0), 'emb', 0, 0, tiled=True)
        cot = permute(n_tiles, slot_col, cot_slots)
        d_tables = backward(n_tiles, lo // BLK, hi // BLK, cot, by_tile[:, None, :], xs, g, ge, ug, w_up, w_down, w_gate, w_proj, range_rows)
        resid_out = jnp.take(back, slot_of, axis=0)
        return resid_out, d_tables

    return jax.shard_map(whole_step, mesh=mesh, in_specs=(tok_spec, act_spec, act_spec, table_spec, full_spec, full_spec, full_spec, full_spec), out_specs=(act_spec, table_spec), check_vma=False)
```

time: 3840 us -> 939 us (0.24)
  waiting for transfers between devices: 2510 us -> 53.7 us
  Pallas kernels: 0 us -> 804 us
  blocking collectives: 377 us -> 0 us
  matrix products: 350 us -> 9.29 us
  local copies, waits for them, and re-layouts: 337 us -> 23.9 us
  other arithmetic: 206 us -> 28 us
    psum x1 -> x0, waiting for transfers between devices: 2490 us -> none  [device_body(): grad_list[l_idx] = lax.psum(shard_grad, 'dp')]
    pallas_call x0 -> x5, Pallas kernels: none -> 804 us  [the longest x1 380 us: backward(): pl.pallas_call(bwd_kernel, grid_spec=pltpu.PrefetchScalarGridSpec(num_sca...]
    all_to_all x5 -> x0, blocking collectives: 377 us -> none  [device_body(): incoming = lax.all_to_all(outgoing, 'emb', 0, 0, tiled=True)]
    dot_general x39 -> x2, matrix products: 350 us -> 9.29 us  [nn(): lax.dot_general(a, b, (((1,), (0,)), ((), ())), preferred_element_type=F32)]
    gather x19 -> x2, local copies, waits for them, and re-layouts: 200 us -> 18.8 us  [the longest x1 12.1 us: whole_step(): jnp.take(x_last, own_pos, axis=0)]
    scatter-add x6 -> x0, other arithmetic: 136 us -> none  [device_body(): jax.ops.segment_sum(incoming, recv_ids, num_segments=range_rows)]
    unnamed x178 -> x12, local copies, waits for them, and re-layouts: 82 us -> 0.03 us
    squeeze x1 -> x0, local copies, waits for them, and re-layouts: 39 us -> none  [device_body(): served = jnp.take(tables[l_idx], recv_ids, axis=0)]
  transfers between devices with their start and end apart: 9 -> 4, of which waited for: 4 -> 1; matrix products, arithmetic and copies ran while one was open for 10% -> 5% of each run, Pallas kernels for 0% -> 86%
where the time goes in v1:
time: 939 us; the launch traced here: 938 us
  Pallas kernels  804 us (86%)
  waiting for transfers between devices  53.7 us (6%)
  other arithmetic  28 us (3%)
  local copies, waits for them, and re-layouts  23.9 us (3%)
  starting transfers between devices  18.4 us (2%)
    pallas_call x1, Pallas kernels, backward(): pl.pallas_call(bwd_kernel, grid_spec=pltpu.PrefetchScalarGridSpec(num_sca...  380 us
    pallas_call x1, Pallas kernels, forward(): pl.pallas_call(fwd_kernel, grid_spec=pltpu.PrefetchScalarGridSpec(num_sca...  312 us
    pallas_call x1, Pallas kernels, gather(): pl.pallas_call(gather_kernel, grid_spec=pltpu.PrefetchScalarGridSpec(num_...  62.8 us
    all_to_all x3, waiting for transfers between devices, exchange(): lax.all_to_all(jnp.concatenate([a] * n_dp, axis=0), ('dp', 'emb'), 0, 0,...  53.7 us
    pallas_call x2, Pallas kernels, permute(): pl.pallas_call(permute_kernel, grid_spec=pltpu.PrefetchScalarGridSpec(num...  48.7 us
  transfers between devices with their start and end apart: 4, of which 1 were waited for; matrix products, arithmetic and copies ran while one was open for 5% of the time, Pallas kernels for 86%

profile of v1, /device:TPU:0, one launch (start us, length us, event | category | flops | bytes accessed | tf_op | source)
XLA Modules:
  0.0 938.5 jit_solution(16720809684679680186)
XLA Ops:
  1.3 2.3 reduce-window.6
  4.2 1.3 compare_and_fusion.1
  7.3 5.3 all-to-all-start
  12.6 5.4 fusion.4
  17.9 3.4 pad_maximum_fusion
  21.3 3.9 all-to-all-start.1
  25.2 3.9 fusion.5
  29.2 3.3 pad_maximum_fusion.1
  33.8 5.8 sort.14
  39.6 3.4 convert_reduce_fusion
  43.1 2.0 copy.21.slot_ref
  45.1 2.0 copy.22.ids_ref
  48.4 53.7 %all-to-all-done.1 = bf16[16,256,768]{2,1,0:T(8,128)(2,1)} async-done(((bf16[16,256,768]{2,1,0:T(8,128)(2,1)}), bf16[16,256,768]{2,1,0:T(8,128)(2,1)}, u32[]{:S(2)}, u32[]{:S(2)}) %all-to-all-start.1) | async-done | bytes 6291488 | tf_op jit(solution)/shard_map/all_to_all | solution.py:410
  102.2 4.5 all-to-all-start.3
  106.7 62.8 %gather.18.refs_1_ = bf16[6,4096,768]{2,1,0:T(8,128)(2,1)} custom-call(s32[1]{0:T(128)} %bitcast.3.n_ref, s32[16]{0:T(128)} %get-tuple-element.27.lo_ref, s32[16]{0:T(128)} %get-tuple-element.25.hi_ref, s32[4096,1]{1,0:T(8,128)} %copy.22.ids_ref, bf16[6,6288,768]{2,1,0:T(8,128)(2,1)} %table_ref.1), custom_call_target="tpu_custom_call" | custom-call | flops 60000002048 | bytes 80000000 | tf_op jit(solution)/shard_map/gather/pallas_call | solution.py:106
  169.5 24.3 %permute.2.refs_0_ = bf16[4096,768]{1,0:T(8,128)(2,1)} custom-call(s32[1]{0:T(128)} %bitcast.3.n_ref, s32[4096,1]{1,0:T(8,128)} %copy.21.slot_ref, bf16[4096,768]{1,0:T(8,128)(2,1)} %bitcast.6.src_ref), custom_call_target="tpu_custom_call" | custom-call | tf_op jit(solution)/shard_map/permute/pallas_call | solution.py:59
  193.8 312.3 %forward.1 = (bf16[6,4096,768]{2,1,0:T(8,128)(2,1)}, f32[6,4096,768]{2,1,0:T(8,128)}, f32[6,4096,768]{2,1,0:T(8,128)}, f32[6,4096,3072]{2,1,0:T(8,128)}, bf16[4096,768]{1,0:T(8,128)(2,1)}) custom-call(s32[1]{0:T(128)} %bitcast.3.n_ref, bf16[4096,768]{1,0:T(8,128)(2,1)} %permute.2.refs_0_, bf16[6,4096,768]{2,1,0:T(8,128)(2,1)} %gather.18.refs_1_, ...), custom_call_target="tpu_custom_call" | custom-call | tf_op jit(solution)/shard_map/forward/pallas_call | solution.py:207
  506.2 12.1 %gather_fusion = bf16[2048,768]{1,0:T(8,128)(2,1)S(1)} fusion(bf16[4096,768]{1,0:T(8,128)(2,1)} %get-tuple-element.10, s32[2048]{0:T(1024)S(1)} %broadcast_clamp_fusion), kind=kCustom, calls=%fused_computation | custom fusion | bytes 6299648 | tf_op jit(solution)/shard_map/jit(_take)/gather | solution.py:432
  518.2 1.9 broadcast_select_fusion
  520.1 4.7 all-to-all-start.2
  526.1 24.4 %permute.3.refs_4_ = bf16[4096,768]{1,0:T(8,128)(2,1)} custom-call(s32[1]{0:T(128)} %bitcast.3.n_ref, s32[4096,1]{1,0:T(8,128)} %copy.21.slot_ref, bf16[4096,768]{1,0:T(8,128)(2,1)} %bitcast.13.src_ref), custom_call_target="tpu_custom_call" | custom-call | tf_op jit(solution)/shard_map/permute/pallas_call | solution.py:59
  550.5 379.8 %backward.1 = f32[6,6288,768]{2,1,0:T(8,128)} custom-call(s32[1]{0:T(128)} %bitcast.3.n_ref, s32[16]{0:T(128)} %copy-done.3, s32[16]{0:T(128)} %copy-done.4, s32[17]{0:T(128)} %get-tuple-element.29.refs_2_, s32[17]{0:T(128)} %get-tuple-element.28.refs_3_, bf16[4096,768]{1,0:T(8,128)(2,1)} %permute.3.refs_4_, s32[16,1,256]{2,1,0:T(1,128)} %bitcast.40, ...), custom_call_target="tpu_custom_call" | custom-call | tf_op jit(solution)/shard_map/backward/pallas_call | solution.py:358
  930.3 6.8 gather_fusion.1
  937.1 1.4 broadcast_select_fusion.1
  (41 shorter events, 6.4 us)
Async XLA Ops:
  7.3 14.0 %all-to-all-start = ((s32[16,256,1]{1,2,0:T(1,128)}), s32[16,256,1]{1,2,0:T(1,128)S(1)}, u32[]{:S(2)}, u32[]{:S(2)}) async-start(s32[16,256,1]{1,2,0:T(1,128)} %copy.20), calls=%async_computation | async-start | bytes 32768 | tf_op jit(solution)/shard_map/all_to_all | solution.py:410
  21.3 3.9 copy-start.5
  21.3 80.8 %all-to-all-start.1 = ((bf16[16,256,768]{2,1,0:T(8,128)(2,1)}), bf16[16,256,768]{2,1,0:T(8,128)(2,1)}, u32[]{:S(2)}, u32[]{:S(2)}) async-start(bf16[16,256,768]{2,1,0:T(8,128)(2,1)} %bitcast.36), calls=%async_computation.1 | async-start | bytes 12582912 | tf_op jit(solution)/shard_map/all_to_all | solution.py:410
  43.1 59.1 %copy-start = (s32[4096]{0:T(1024)}, s32[4096]{0:T(1024)S(1)}, u32[]{:S(2)}) copy-start(s32[4096]{0:T(1024)S(1)} %get-tuple-element.17) | copy-start | bytes 49156
  47.8 477.6 %copy-start.3 = (s32[16]{0:T(128)}, s32[16]{0:T(128)S(1)}, u32[]{:S(2)}) copy-start(s32[16]{0:T(128)S(1)} %get-tuple-element.26.refs_0_) | copy-start | bytes 196
  48.4 477.0 %copy-start.4 = (s32[16]{0:T(128)}, s32[16]{0:T(128)S(1)}, u32[]{:S(2)}) copy-start(s32[16]{0:T(128)S(1)} %get-tuple-element.24.refs_1_) | copy-start | bytes 196
  102.2 418.0 %all-to-all-start.3 = ((bf16[16,256,768]{2,1,0:T(8,128)(2,1)}), bf16[16,256,768]{2,1,0:T(8,128)(2,1)}, u32[]{:S(2)}, u32[]{:S(2)}) async-start(bf16[16,256,768]{2,1,0:T(8,128)(2,1)} %bitcast.37), calls=%async_computation.3 | async-start | bytes 12582912 | tf_op jit(solution)/shard_map/all_to_all | solution.py:410
  520.1 410.2 %all-to-all-start.2 = ((bf16[8,256,768]{2,1,0:T(8,128)(2,1)}), bf16[8,256,768]{2,1,0:T(8,128)(2,1)}, u32[]{:S(2)}, u32[]{:S(2)}) async-start(bf16[8,256,768]{2,1,0:T(8,128)(2,1)} %broadcast_select_fusion), calls=%async_computation.2 | async-start | bytes 6291456 | tf_op jit(solution)/shard_map/all_to_all | solution.py:432
  550.5 379.8 %copy-start.1 = (s32[1024]{0:T(1024)S(1)}, s32[1024]{0:T(1024)}, u32[]{:S(2)}) copy-start(s32[1024]{0:T(1024)} %fusion.15) | copy-start | bytes 12292
  930.3 6.8 copy-start.2

commit v2 on v1

--- a/solution.py
+++ b/solution.py
@@ -12,6 +12,8 @@
 TILE = 256
 BLK = 256
 GBLK = 512
+PCH = 2048
+SUB = 2
 FCH = 768
 F32 = jnp.float32
 BF16 = jnp.bfloat16
@@ -20,10 +22,10 @@
 
 def gelu_and_grad(x):
     x2 = x * x
-    t = jnp.tanh(x * (GELU_C + (GELU_C * GELU_A) * x2))
-    h = 0.5 + 0.5 * t
-    grad = h + (0.5 * x) * (1.0 - t * t) * (GELU_C + (3.0 * GELU_C * GELU_A) * x2)
-    return x * h, grad
+    h = 0.5 + 0.5 * jnp.tanh(x * (GELU_C + (GELU_C * GELU_A) * x2))
+    y = x * h
+    grad = h + (y - y * h) * (2.0 * GELU_C + (6.0 * GELU_C * GELU_A) * x2)
+    return y, grad
 
 
 def nn(a, b):
@@ -44,13 +46,15 @@
     @pl.when(pl.program_id(0) < n_ref[0])
     def _():
         slot = slot_ref[...]
-        chunk = 512
-        acc_ref[...] = jnp.zeros_like(acc_ref)
-        for c in range(n_slots // chunk):
-            cols = lax.broadcasted_iota(jnp.int32, (TILE, chunk), 1) + c * chunk
+        for c in range(n_slots // PCH):
+            cols = lax.broadcasted_iota(jnp.int32, (TILE, PCH), 1) + c * PCH
             sel = jnp.where(slot == cols, 1.0, 0.0).astype(BF16)
-            acc_ref[...] += nn(sel, src_ref[c * chunk:(c + 1) * chunk, :])
-        out_ref[...] = acc_ref[...].astype(BF16)
+            part = nn(sel, src_ref[c * PCH:(c + 1) * PCH, :])
+            acc = part if c == 0 else acc_ref[...] + part
+            if c == n_slots // PCH - 1:
+                out_ref[...] = acc.astype(BF16)
+            else:
+                acc_ref[...] = acc
 
 
 def permute(n_tiles, slot_col, src):
@@ -153,72 +157,75 @@
     ]
 
 
-def fwd_kernel(n_ref, *refs):
-    @pl.when(pl.program_id(1) < n_ref[0])
-    def _():
-        fwd_tile(*refs)
-
-
-def fwd_tile(x0_ref, e_ref, w_up, w_down, w_gate, w_proj, xs_ref, g_ref, ge_ref, ug_ref, xl_ref,
-             x_scr, m_scr, up_buf, down_buf, gate_buf, proj_buf, w_sems):
+def fwd_kernel(n_ref, x0_ref, e_ref, w_up, w_down, w_gate, w_proj, xs_ref, g_ref, ge_ref, ug_ref, xl_ref,
+               x_scr, m_scr, up_buf, down_buf, gate_buf, proj_buf, w_sems):
     l = pl.program_id(0)
     i = pl.program_id(1)
     n_layers = pl.num_programs(0)
     slot = lax.rem(l, 2)
-    rows = pl.ds(pl.multiple_of(i * TILE, TILE), TILE)
 
     @pl.when(i == 0)
     def _():
         next_weights((w_up, w_down, w_gate, w_proj), (up_buf, down_buf, gate_buf, proj_buf), w_sems, l, n_layers, lambda q: q)
 
-    @pl.when(l == 0)
-    def _():
-        x_scr[rows, :] = x0_ref[...]
-
-    x = x_scr[rows, :]
-    xs_ref[0] = x
-    xf = x.astype(F32)
-    u = (xf * norm_stats(xf)).astype(BF16)
-    gate, gate_grad = gelu_and_grad(nn(u, gate_buf[slot]))
-    emb = e_ref[0].astype(F32)
-    g_ref[0] = gate
-    ge_ref[0] = gate_grad * emb
-    m_scr[...] = xf + nn((gate * emb).astype(BF16), proj_buf[slot])
-    ffn = up_buf.shape[2]
-    for c in range(ffn // FCH):
-        cs = slice(c * FCH, (c + 1) * FCH)
-        hid, hid_grad = gelu_and_grad(nn(u, up_buf[slot, :, cs]))
-        ug_ref[0, :, cs] = hid_grad
-        m_scr[...] += nn(hid.astype(BF16), down_buf[slot, cs, :])
-    x_next = m_scr[...].astype(BF16)
-    x_scr[rows, :] = x_next
-
-    @pl.when(l == n_layers - 1)
-    def _():
-        xl_ref[...] = x_next
+    def sub_tile(h, carry):
+        here = pl.ds(pl.multiple_of(h * TILE, TILE), TILE)
+        rows = pl.ds(pl.multiple_of((i * SUB + h) * TILE, TILE), TILE)
+
+        @pl.when(l == 0)
+        def _():
+            x_scr[rows, :] = x0_ref[here, :]
+
+        x = x_scr[rows, :]
+        xs_ref[0, here, :] = x
+        xf = x.astype(F32)
+        u = (xf * norm_stats(xf)).astype(BF16)
+        gate, gate_grad = gelu_and_grad(nn(u, gate_buf[slot]))
+        emb = e_ref[0, here, :].astype(F32)
+        g_ref[0, here, :] = gate
+        ge_ref[0, here, :] = gate_grad * emb
+        m_scr[...] = xf + nn((gate * emb).astype(BF16), proj_buf[slot])
+        ffn = up_buf.shape[2]
+        for c in range(ffn // FCH):
+            cs = slice(c * FCH, (c + 1) * FCH)
+            hid, hid_grad = gelu_and_grad(nn(u, up_buf[slot, :, cs]))
+            ug_ref[0, here, cs] = hid_grad
+            m_scr[...] += nn(hid.astype(BF16), down_buf[slot, cs, :])
+        x_next = m_scr[...].astype(BF16)
+        x_scr[rows, :] = x_next
+
+        @pl.when(l == n_layers - 1)
+        def _():
+            xl_ref[here, :] = x_next
+
+        return carry
+
+    lax.fori_loop(0, jnp.clip(n_ref[0] - i * SUB, 0, SUB), sub_tile, 0)
 
 
 def forward(n_tiles, x0, es, w_up, w_down, w_gate, w_proj):
     n_layers, n_slots, e = es.shape
     d = x0.shape[1]
     ffn = w_up.shape[2]
-    tile = lambda l, i, n: (l, jnp.minimum(i, n[0] - 1), 0)
-    only = lambda which: (lambda l, i, n: (jnp.where(l == which, jnp.minimum(i, n[0] - 1), 0), 0))
+    step = SUB * TILE
+    last = lambda i, n: jnp.minimum(i, (n[0] + SUB - 1) // SUB - 1)
+    tile = lambda l, i, n: (l, last(i, n), 0)
+    only = lambda which: (lambda l, i, n: (jnp.where(l == which, last(i, n), 0), 0))
     return pl.pallas_call(
         fwd_kernel,
         grid_spec=pltpu.PrefetchScalarGridSpec(
             num_scalar_prefetch=1,
-            grid=(n_layers, n_slots // TILE),
+            grid=(n_layers, n_slots // step),
             in_specs=[
-                pl.BlockSpec((TILE, d), only(0)),
-                pl.BlockSpec((1, TILE, e), tile),
+                pl.BlockSpec((step, d), only(0)),
+                pl.BlockSpec((1, step, e), tile),
             ] + [pl.BlockSpec(memory_space=pl.ANY)] * 4,
             out_specs=[
-                pl.BlockSpec((1, TILE, d), tile),
-                pl.BlockSpec((1, TILE, e), tile),
-                pl.BlockSpec((1, TILE, e), tile),
-                pl.BlockSpec((1, TILE, ffn), tile),
-                pl.BlockSpec((TILE, d), only(n_layers - 1)),
+                pl.BlockSpec((1, step, d), tile),
+                pl.BlockSpec((1, step, e), tile),
+                pl.BlockSpec((1, step, e), tile),
+                pl.BlockSpec((1, step, ffn), tile),
+                pl.BlockSpec((step, d), only(n_layers - 1)),
             ],
             scratch_shapes=[
                 pltpu.VMEM((n_slots, d), BF16),
@@ -320,23 +327,37 @@
 
     ids = ids_ref[0]
 
-    def scatter_step(b, carry):
-        pos = lax.broadcasted_iota(jnp.int32, (BLK, TILE), 0) + b * BLK
+    def sums(b, blocks):
+        pos = lax.broadcasted_iota(jnp.int32, (blocks * BLK, TILE), 0) + b * BLK
         sel = jnp.where(ids == pos, 1.0, 0.0).astype(BF16)
-        part = nn(jnp.concatenate([sel, sel, sel], axis=1), parts_scr[...])
-        at = pl.ds(pl.multiple_of(b * BLK, BLK), BLK)
-
-        @pl.when(b >= fresh)
-        def _():
-            acc[at, :] = part
-
-        @pl.when(b < fresh)
-        def _():
-            acc[at, :] += part
-
+        return nn(jnp.concatenate([sel, sel, sel], axis=1), parts_scr[...])
+
+    def at(b, blocks):
+        return pl.ds(pl.multiple_of(b * BLK, BLK), blocks * BLK)
+
+    first = lo_ref[i]
+    more = hi_ref[i] - first
+    head = sums(first, 1)
+
+    @pl.when(first >= fresh)
+    def _():
+        acc[at(first, 1), :] = head
+
+    @pl.when(first < fresh)
+    def _():
+        acc[at(first, 1), :] += head
+
+    def two_blocks(k, carry):
+        b = first + 1 + 2 * k
+        acc[at(b, 2), :] = sums(b, 2)
         return carry
 
-    lax.fori_loop(lo_ref[i], hi_ref[i] + 1, scatter_step, 0)
+    lax.fori_loop(0, more // 2, two_blocks, 0)
+
+    @pl.when(lax.rem(more, 2) == 1)
+    def _():
+        acc[at(first + more, 1), :] = sums(first + more, 1)
+
     each_block(cs_ref[i], cs_ref[i + 1], lambda c: c.start())
 
     @pl.when((l == 0) & (i == n_tiles - 1))
@@ -411,7 +432,8 @@
 
         recv_ids = exchange(slot_ids)
         x_slots = exchange(nn(sel, resid_in).astype(BF16))
-        cot_slots = exchange(nn(sel, cot_out).astype(BF16))
+        cot_send = nn(sel, cot_out).astype(BF16)
+        cot_slots = exchange(cot_send)
 
         raw_key = recv_ids * n_slots + jnp.arange(n_slots, dtype=jnp.int32)
         key = lax.sort(raw_key)
@@ -429,10 +451,10 @@
         es = gather(n_tiles, lo // GBLK, hi // GBLK, ids_sorted[:, None], tables)
         x0 = permute(n_tiles, slot_col, x_slots)
         xs, g, ge, ug, x_last = forward(n_tiles, x0, es, w_up, w_down, w_gate, w_proj)
-        back = lax.all_to_all(jnp.take(x_last, own_pos, axis=0), 'emb', 0, 0, tiled=True)
+        back = lax.all_to_all(x_last.at[own_pos].get(mode="promise_in_bounds"), 'emb', 0, 0, tiled=True)
         cot = permute(n_tiles, slot_col, cot_slots)
         d_tables = backward(n_tiles, lo // BLK, hi // BLK, cot, by_tile[:, None, :], xs, g, ge, ug, w_up, w_down, w_gate, w_proj, range_rows)
-        resid_out = jnp.take(back, slot_of, axis=0)
+        resid_out = back.at[slot_of].get(mode="promise_in_bounds")
         return resid_out, d_tables
 
     return jax.shard_map(whole_step, mesh=mesh, in_specs=(tok_spec, act_spec, act_spec, table_spec, full_spec, full_spec, full_spec, full_spec), out_specs=(act_spec, table_spec), check_vma=False)

time: 939 us -> 913 us (0.972)
  Pallas kernels: 804 us -> 773 us
    pallas_call x1, Pallas kernels: 312 us -> 294 us  [forward(): pl.pallas_call(fwd_kernel, grid_spec=pltpu.PrefetchScalarGridSpec(num_sca...]
    pallas_call x1, Pallas kernels: 380 us -> 368 us  [backward(): pl.pallas_call(bwd_kernel, grid_spec=pltpu.PrefetchScalarGridSpec(num_sca...]
  transfers between devices with their start and end apart: 4 -> 4, of which waited for: 1 -> 1; matrix products, arithmetic and copies ran while one was open for 5% -> 5% of each run, Pallas kernels for 86% -> 85%
where the time goes in v2:
time: 913 us; the launch traced here: 912 us
  Pallas kernels  773 us (85%)
  waiting for transfers between devices  58.9 us (6%)
  local copies, waits for them, and re-layouts  26.5 us (3%)
  other arithmetic  24.2 us (3%)
  starting transfers between devices  18.4 us (2%)
  matrix products  9.31 us (1%)
    pallas_call x1, Pallas kernels, backward(): pl.pallas_call(bwd_kernel, grid_spec=pltpu.PrefetchScalarGridSpec(num_sca...  368 us
    pallas_call x1, Pallas kernels, forward(): pl.pallas_call(fwd_kernel, grid_spec=pltpu.PrefetchScalarGridSpec(num_sca...  294 us
    pallas_call x1, Pallas kernels, gather(): pl.pallas_call(gather_kernel, grid_spec=pltpu.PrefetchScalarGridSpec(num_...  62.8 us
    all_to_all x3, waiting for transfers between devices, exchange(): lax.all_to_all(jnp.concatenate([a] * n_dp, axis=0), ('dp', 'emb'), 0, 0,...  58.9 us
    pallas_call x2, Pallas kernels, permute(): pl.pallas_call(permute_kernel, grid_spec=pltpu.PrefetchScalarGridSpec(num...  48.5 us
  transfers between devices with their start and end apart: 4, of which 1 were waited for; matrix products, arithmetic and copies ran while one was open for 5% of the time, Pallas kernels for 85%

profile of v2, /device:TPU:0, one launch (start us, length us, event | category | flops | bytes accessed | tf_op | source)
XLA Modules:
  0.0 912.0 jit_solution(6719732919420331955)
XLA Ops:
  1.3 2.3 reduce-window.6
  4.2 1.3 fusion.14
  5.5 1.2 select_reduce_fusion
  7.3 5.3 all-to-all-start
  12.6 5.3 fusion.4
  17.9 3.4 pad_maximum_fusion
  21.3 3.9 all-to-all-start.1
  25.2 4.0 fusion.5
  29.2 3.3 pad_maximum_fusion.1
  32.5 0.7 broadcast_multiply_fusion
  33.3 5.8 sort.14
  39.9 3.4 convert_reduce_fusion
  43.3 58.9 %all-to-all-done.1 = bf16[16,256,768]{2,1,0:T(8,128)(2,1)} async-done(((bf16[16,256,768]{2,1,0:T(8,128)(2,1)}), bf16[16,256,768]{2,1,0:T(8,128)(2,1)}, u32[]{:S(2)}, u32[]{:S(2)}) %all-to-all-start.1) | async-done | bytes 6291488 | tf_op jit(solution)/shard_map/all_to_all | solution.py:431
  102.2 4.5 all-to-all-start.3
  108.0 2.0 copy.21.slot_ref
  110.0 2.0 copy.22.ids_ref
  111.9 62.8 %gather.13.e_ref = bf16[6,4096,768]{2,1,0:T(8,128)(2,1)} custom-call(s32[1]{0:T(128)} %bitcast.2.n_ref, s32[16]{0:T(128)} %get-tuple-element.27.lo_ref, s32[16]{0:T(128)} %get-tuple-element.25.hi_ref, s32[4096,1]{1,0:T(8,128)} %copy.22.ids_ref, bf16[6,6288,768]{2,1,0:T(8,128)(2,1)} %table_ref.1), custom_call_target="tpu_custom_call" | custom-call | flops 60000002048 | bytes 80000000 | tf_op jit(solution)/shard_map/gather/pallas_call | solution.py:110
  174.7 24.3 %permute.2.x0_ref = bf16[4096,768]{1,0:T(8,128)(2,1)} custom-call(s32[1]{0:T(128)} %bitcast.2.n_ref, s32[4096,1]{1,0:T(8,128)} %copy.21.slot_ref, bf16[4096,768]{1,0:T(8,128)(2,1)} %bitcast.6.src_ref), custom_call_target="tpu_custom_call" | custom-call | tf_op jit(solution)/shard_map/permute/pallas_call | solution.py:63
  199.0 294.1 %forward.1 = (bf16[6,4096,768]{2,1,0:T(8,128)(2,1)}, f32[6,4096,768]{2,1,0:T(8,128)}, f32[6,4096,768]{2,1,0:T(8,128)}, f32[6,4096,3072]{2,1,0:T(8,128)}, bf16[4096,768]{1,0:T(8,128)(2,1)}) custom-call(s32[1]{0:T(128)} %bitcast.2.n_ref, bf16[4096,768]{1,0:T(8,128)(2,1)} %permute.2.x0_ref, bf16[6,4096,768]{2,1,0:T(8,128)(2,1)} %gather.13.e_ref, ...), custom_call_target="tpu_custom_call" | custom-call | tf_op jit(solution)/shard_map/forward/pallas_call | solution.py:214
  493.1 13.7 %gather_fusion = bf16[2048,768]{1,0:T(8,128)(2,1)} fusion(bf16[4096,768]{1,0:T(8,128)(2,1)} %get-tuple-element.10, s32[2048]{0:T(1024)S(1)} %broadcast_clamp_fusion), kind=kCustom, calls=%fused_computation | custom fusion | bytes 6299648 | tf_op jit(solution)/shard_map/gather | solution.py:454
  506.8 4.7 all-to-all-start.2
  512.1 24.3 %permute.3.refs_4_ = bf16[4096,768]{1,0:T(8,128)(2,1)} custom-call(s32[1]{0:T(128)} %bitcast.2.n_ref, s32[4096,1]{1,0:T(8,128)} %copy.21.slot_ref, bf16[4096,768]{1,0:T(8,128)(2,1)} %bitcast.13.src_ref), custom_call_target="tpu_custom_call" | custom-call | tf_op jit(solution)/shard_map/permute/pallas_call | solution.py:63
  536.4 367.8 %backward.1 = f32[6,6288,768]{2,1,0:T(8,128)} custom-call(s32[1]{0:T(128)} %bitcast.2.n_ref, s32[16]{0:T(128)} %copy-done.2, s32[16]{0:T(128)} %copy-done.3, s32[17]{0:T(128)} %get-tuple-element.29.refs_2_, s32[17]{0:T(128)} %get-tuple-element.28.refs_3_, bf16[4096,768]{1,0:T(8,128)(2,1)} %permute.3.refs_4_, s32[16,1,256]{2,1,0:T(1,128)} %bitcast.39, ...), custom_call_target="tpu_custom_call" | custom-call | tf_op jit(solution)/shard_map/backward/pallas_call | solution.py:379
  904.2 7.9 gather_fusion.1
  (34 shorter events, 3.9 us)
Async XLA Ops:
  7.3 14.0 %all-to-all-start = ((s32[16,256,1]{1,2,0:T(1,128)}), s32[16,256,1]{1,2,0:T(1,128)S(1)}, u32[]{:S(2)}, u32[]{:S(2)}) async-start(s32[16,256,1]{1,2,0:T(1,128)} %copy.20), calls=%async_computation | async-start | bytes 32768 | tf_op jit(solution)/shard_map/all_to_all | solution.py:431
  21.3 3.9 copy-start.4
  21.3 80.8 %all-to-all-start.1 = ((bf16[16,256,768]{2,1,0:T(8,128)(2,1)}), bf16[16,256,768]{2,1,0:T(8,128)(2,1)}, u32[]{:S(2)}, u32[]{:S(2)}) async-start(bf16[16,256,768]{2,1,0:T(8,128)(2,1)} %bitcast.37), calls=%async_computation.1 | async-start | bytes 12582912 | tf_op jit(solution)/shard_map/all_to_all | solution.py:431
  39.1 70.9 %copy-start = (s32[4096]{0:T(1024)}, s32[4096]{0:T(1024)S(1)}, u32[]{:S(2)}) copy-start(s32[4096]{0:T(1024)S(1)} %get-tuple-element.17) | copy-start | bytes 49156
  39.9 471.7 %copy-start.2 = (s32[16]{0:T(128)}, s32[16]{0:T(128)S(1)}, u32[]{:S(2)}) copy-start(s32[16]{0:T(128)S(1)} %get-tuple-element.26.refs_0_) | copy-start | bytes 196
  102.2 404.6 %all-to-all-start.3 = ((bf16[16,256,768]{2,1,0:T(8,128)(2,1)}), bf16[16,256,768]{2,1,0:T(8,128)(2,1)}, u32[]{:S(2)}, u32[]{:S(2)}) async-start(bf16[16,256,768]{2,1,0:T(8,128)(2,1)} %bitcast.36), calls=%async_computation.3 | async-start | bytes 12582912 | tf_op jit(solution)/shard_map/all_to_all | solution.py:431
  107.3 404.3 %copy-start.3 = (s32[16]{0:T(128)}, s32[16]{0:T(128)S(1)}, u32[]{:S(2)}) copy-start(s32[16]{0:T(128)S(1)} %get-tuple-element.24.refs_1_) | copy-start | bytes 196
  506.8 397.4 %all-to-all-start.2 = ((bf16[8,256,768]{2,1,0:T(8,128)(2,1)}), bf16[8,256,768]{2,1,0:T(8,128)(2,1)}, u32[]{:S(2)}, u32[]{:S(2)}) async-start(bf16[8,256,768]{2,1,0:T(8,128)(2,1)} %bitcast.10), calls=%async_computation.2 | async-start | bytes 6291456 | tf_op jit(solution)/shard_map/all_to_all | solution.py:454
  536.4 367.8 %copy-start.1 = (s32[1024]{0:T(1024)S(1)}, s32[1024]{0:T(1024)}, u32[]{:S(2)}) copy-start(s32[1024]{0:T(1024)} %get-tuple-element.15) | copy-start | bytes 12292
